TPU v7x, 32 devices: a whole 2x2x4 slice. The times are simulated.
32 devices in a mesh: groups: 2 (over x), expert: 16 (over z, y, core).
Axes of the slice: x: 2, y: 2, z: 4, core: 2. Of those that a mesh axis runs over, the one named last changes fastest.
Arguments:
- tokens: bfloat16 [1024, 2048], P(('groups', 'expert')), parts along dimension 0, may hold values from -6 to 6
- expert_ids: int32 [1024, 2], P(('groups', 'expert')), parts along dimension 0, may hold values from 0 to 7, all different within a row; in each aligned block of 32 rows (0 to 31, 32 to 63, ...) at most 16 rows name the same one
- member_ids: int32 [1024], P(('groups', 'expert')), parts along dimension 0, may hold values from 0 to 7
- combine_weights: float32 [1024, 2], P(('groups', 'expert')), parts along dimension 0, may hold values from 0.25 to 1
- gate_weight: bfloat16 [2048, 57344], P(None, 'expert'), may hold values from -0.125 to 0.125
- up_weight: bfloat16 [2048, 57344], P(None, 'expert'), may hold values from -0.125 to 0.125
- down_weight: bfloat16 [57344, 2048], P('expert'), may hold values from -0.0625 to 0.0625
- input_factors: float32 [8, 8, 4096], replicated, may hold values from 0.5 to 2
- hidden_factors: float32 [8, 2, 57344], P(None, None, 'expert'), may hold values from 0.5 to 2
- output_factors: float32 [8, 8, 2048], replicated, may hold values from 0.5 to 2
Outputs:
- mixed: bfloat16 [1024, 2048], P(('groups', 'expert')), parts along dimension 0
There are 2 independent parts, one for each index of `groups`. A program takes and returns all parts, laid end to end along the dimension named above; an argument that names none is the same for every part. Nothing has to cross between parts.
Inputs may be any that keep to these rules, and one draw needn't show every extreme that they name: `expert_ids`: the two experts of a token differ. Among the 32 tokens of one device no expert is named more than 16 times.
All inputs are finite; a program needn't handle non-finite values.
Results may differ from a plain program's by a relative error of at most 0.012.
Values may be sent and summed in bfloat16 or wider, within the bound.
No kernel may reach another device: no remote copies, remote signals or barrier semaphores. Data moves between devices by JAX's collectives and lax.ppermute only.
A program may use at most 128 MiB of HBM per device.

v0:
```python
import jax
import jax.numpy as jnp
from jax import lax
from jax.sharding import PartitionSpec as P

EXPERTS = 8
MEMBERS = 8
CAP = 16


def swapped(block, axis, apart):
    count = lax.axis_size(axis)
    route = []
    for low in range(count):
        high = low | 1 << apart
        if high != low and high < count:
            route += [(low, high), (high, low)]
    return lax.ppermute(block, axis, route)


def lookup(select, table):
    return jnp.dot(
        select, table, precision=lax.Precision.HIGHEST, preferred_element_type=jnp.float32
    )


def expert_rows(
    row_data,
    plus_member,
    own_expert,
    gate_weight,
    up_weight,
    down_weight,
    input_factors,
    hidden_factors,
):
    members = input_factors.shape[1]
    width = row_data.shape[1]
    units = gate_weight.shape[1]
    select = (
        plus_member.astype(jnp.float32)[:, None] - 1.0
        == jnp.arange(members, dtype=jnp.float32)[None, :]
    ).astype(jnp.float32)
    in_table = lax.dynamic_index_in_dim(input_factors, own_expert, 0, keepdims=False)
    in_scale = lookup(select, in_table)
    gate_in = (row_data * in_scale[:, :width]).astype(jnp.bfloat16)
    up_in = (row_data * in_scale[:, width:]).astype(jnp.bfloat16)
    gate = jnp.dot(gate_in, gate_weight, preferred_element_type=jnp.float32)
    up = jnp.dot(up_in, up_weight, preferred_element_type=jnp.float32)
    hid_scale = lookup(select, hidden_factors.reshape(members, 2 * units))
    hidden = (jax.nn.silu(gate * hid_scale[:, :units]) * (up * hid_scale[:, units:])).astype(
        jnp.bfloat16
    )
    return jnp.dot(hidden, down_weight, preferred_element_type=jnp.float32).astype(jnp.bfloat16)


def run_rows(
    row_data,
    plus_member,
    own_expert,
    gate_weight,
    up_weight,
    down_weight,
    input_factors,
    hidden_factors,
):
    return expert_rows(
        row_data,
        plus_member,
        own_expert,
        gate_weight,
        up_weight,
        down_weight,
        input_factors,
        hidden_factors,
    )


def send_back(partial_value, position, split):
    devices = partial_value.shape[0]
    slots = partial_value.shape[1]
    width = partial_value.shape[2]
    held = partial_value.astype(jnp.float32)
    levels = split.bit_length() - 1
    for level in range(levels):
        bit = levels - 1 - level
        half = held.shape[1] // 2
        lower = held[:, :half]
        higher = held[:, half:]
        upper = position // 2**bit % 2 == 1
        keep = jnp.where(upper, higher, lower)
        give = jnp.where(upper, lower, higher)
        held = keep + swapped(give.astype(jnp.bfloat16), "expert", bit).astype(give.dtype)
    arrived = lax.all_to_all(
        held.astype(jnp.bfloat16), "expert", split_axis=0, concat_axis=0, tiled=True
    ).astype(held.dtype)
    return arrived.reshape(devices // split * slots, width)


def per_device(
    tokens,
    expert_ids,
    member_ids,
    combine_weights,
    gate_weight,
    up_weight,
    down_weight,
    input_factors,
    hidden_factors,
    output_factors,
):
    devices = lax.axis_size("expert")
    split = devices // EXPERTS
    position = lax.axis_index("expert")
    own_expert = position // split
    tok_count = tokens.shape[0]
    width = tokens.shape[1]
    flat_expert = expert_ids.reshape(-1)
    expert_hits = (flat_expert[:, None] == jnp.arange(EXPERTS, dtype=jnp.int32)[None, :]).astype(
        jnp.int32
    )
    slot_index = jnp.sum((jnp.cumsum(expert_hits, 0) - 1) * expert_hits, 1)
    target = flat_expert * CAP + slot_index
    placing = (jnp.arange(EXPERTS * CAP, dtype=jnp.int32)[:, None] == target[None, :]).astype(
        jnp.float32
    )
    by_token = placing.reshape(EXPERTS * CAP, tok_count, 2).sum(2)
    send_rows = jnp.dot(
        by_token.astype(jnp.bfloat16), tokens, preferred_element_type=jnp.float32
    ).astype(jnp.bfloat16)
    send_member = jnp.dot(
        by_token, (member_ids + 1).astype(jnp.float32), precision=lax.Precision.HIGHEST
    ).astype(jnp.bfloat16)
    rows_out = jnp.repeat(send_rows.reshape(EXPERTS, CAP, width), split, axis=0)
    member_out = jnp.repeat(send_member.reshape(EXPERTS, CAP, 1), split, axis=0)
    row_piece, member_piece = (
        lax.all_to_all(rows_out, "expert", split_axis=0, concat_axis=0, tiled=True),
        lax.all_to_all(member_out, "expert", split_axis=0, concat_axis=0, tiled=True),
    )
    partial_value = run_rows(
        row_piece.reshape(devices * CAP, width),
        member_piece.reshape(devices * CAP),
        own_expert,
        gate_weight,
        up_weight,
        down_weight,
        input_factors,
        hidden_factors,
    )
    summed = send_back(partial_value.reshape(devices, CAP, width), position, split)
    picked = jnp.dot(
        placing.T, summed, precision=lax.Precision.HIGHEST, preferred_element_type=jnp.float32
    )
    pair_member = jnp.repeat(member_ids, 2)
    factor_hits = (
        (flat_expert * MEMBERS + pair_member)[:, None]
        == jnp.arange(EXPERTS * MEMBERS, dtype=jnp.int32)[None, :]
    ).astype(jnp.float32)
    out_scale = lookup(factor_hits, output_factors.reshape(EXPERTS * MEMBERS, width))
    weighted = picked * out_scale * combine_weights.reshape(-1)[:, None]
    return weighted.reshape(tok_count, 2, width).sum(1).astype(jnp.bfloat16)


def solution(mesh):
    in_specs = (
        P(("groups", "expert"), None),
        P(("groups", "expert"), None),
        P(("groups", "expert")),
        P(("groups", "expert"), None),
        P(None, "expert"),
        P(None, "expert"),
        P("expert", None),
        P(),
        P(None, None, "expert"),
        P(),
    )
    out_specs = P(("groups", "expert"), None)
    return jax.shard_map(
        per_device, mesh=mesh, in_specs=in_specs, out_specs=out_specs, check_vma=False
    )
```

profile of v0, /device:TPU:0, one launch (start us, length us, event | category | flops | bytes accessed | tf_op | source)
XLA Modules:
  0.0 101.5 jit_solution(2548334407414446849)
XLA Ops:
  0.0 0.9 copy.34
  1.5 0.7 multiply_add_fusion
  2.3 0.8 fusion.5
  3.2 0.6 copy.36
  3.8 7.4 %all-to-all-start.1 = ((bf16[16,16,1]{1,2,0:T(2,128)(2,1)}), bf16[16,16,1]{1,2,0:T(2,128)(2,1)S(1)}, u32[]{:S(2)}, u32[]{:S(2)}) async-start(bf16[16,16,1]{1,2,0:T(2,128)(2,1)} %copy.36), calls=%async_computation.1 | async-start | bytes 16384 | tf_op jit(solution)/shard_map/all_to_all | solution.py:138
  11.2 1.2 %convolution_convert_fusion.1 = bf16[128,2048]{1,0:T(8,128)(2,1)S(1)} fusion(bf16[32,2048]{1,0:T(8,128)(2,1)} %param.10, f32[128,32]{0,1:T(8,128)S(1)} %convert_reduce_fusion), kind=kOutput, calls=%fused_computation.7 | convolution fusion | flops 17043456 | bytes 671744 | tf_op jit(solution)/shard_map/dot_general | solution.py:128
  12.5 5.1 %all-to-all-done.1 = bf16[16,16,1]{1,2,0:T(2,128)(2,1)S(1)} async-done(((bf16[16,16,1]{1,2,0:T(2,128)(2,1)}), bf16[16,16,1]{1,2,0:T(2,128)(2,1)S(1)}, u32[]{:S(2)}, u32[]{:S(2)}) %all-to-all-start.1) | async-done | bytes 544 | tf_op jit(solution)/shard_map/all_to_all | solution.py:138
  17.6 1.1 %broadcast_in_dim.8 = bf16[8,2,16,2048]{3,2,1,0:T(8,128)(2,1)} broadcast(bf16[8,16,2048]{2,1,0:T(8,128)(2,1)S(1)} %bitcast.31), dimensions={0,2,3} | broadcast | bytes 1572864 | tf_op jit(solution)/shard_map/broadcast_in_dim | solution.py:134
  18.7 3.7 %all-to-all-start = ((bf16[16,16,2048]{2,1,0:T(8,128)(2,1)}), bf16[16,16,2048]{2,1,0:T(8,128)(2,1)S(1)}, u32[]{:S(2)}, u32[]{:S(2)}) async-start(bf16[16,16,2048]{2,1,0:T(8,128)(2,1)} %bitcast.1), calls=%async_computation | async-start | bytes 2097152 | tf_op jit(solution)/shard_map/all_to_all | solution.py:137
  22.5 3.9 %fusion.13 = f32[256,4096]{1,0:T(8,128)} fusion(f32[8,8,4096]{2,1,0:T(8,128)S(1)} %copy-done, s32[]{:T(128)S(6)} %select_n.31, f32[256]{0:T(256)S(1)} %sub.17), kind=kOutput, calls=%fused_computation.19 | convolution fusion | flops 100665344 | bytes 4326404 | tf_op jit(solution)/shard_map/dot_general | solution.py:22
  26.5 5.1 %fusion.16 = f32[256,7168]{1,0:T(8,128)} fusion(f32[8,7168]{1,0:T(8,128)S(1)} %bitcast.35, f32[256]{0:T(256)S(1)} %sub.17), kind=kOutput, calls=%fused_computation.23 | convolution fusion | flops 176162816 | bytes 7570432 | tf_op jit(solution)/shard_map/dot_general | solution.py:22
  31.6 13.6 %all-to-all-done = bf16[16,16,2048]{2,1,0:T(8,128)(2,1)S(1)} async-done(((bf16[16,16,2048]{2,1,0:T(8,128)(2,1)}), bf16[16,16,2048]{2,1,0:T(8,128)(2,1)S(1)}, u32[]{:S(2)}, u32[]{:S(2)}) %all-to-all-start) | async-done | bytes 1048608 | tf_op jit(solution)/shard_map/all_to_all | solution.py:137
  45.2 12.7 %convolution_multiply_fusion.1 = f32[256,3584]{1,0:T(8,128)} fusion(bf16[2048,3584]{1,0:T(8,128)(2,1)} %param.14, f32[256,7168]{1,0:T(8,128)} %fusion.16, bf16[256,2048]{1,0:T(8,128)(2,1)S(1)} %bitcast.33, f32[256,4096]{1,0:T(8,128)} %fusion.13), kind=kOutput, calls=%fused_computation.2 | convolution fusion | flops 3760586752 | bytes 25165824 | tf_op jit(solution)/shard_map/dot_general | solution.py:48
  57.9 16.9 %convolution_convert_fusion = bf16[256,2048]{1,0:T(8,128)(2,1)S(1)} fusion(bf16[3584,2048]{1,0:T(8,128)(2,1)} %param.16, bf16[2048,3584]{1,0:T(8,128)(2,1)} %param.15, f32[256,7168]{1,0:T(8,128)} %fusion.16, f32[256,3584]{1,0:T(8,128)} %convolution_multiply_fusion.1, bf16[256,2048]{1,0:T(8,128)(2,1)S(1)} %bitcast.34, f32[256,4096]{1,0:T(8,128)} %fusion.13), kind=kOutput, calls=%fused_computation.6 | convolution fusion | flops 7524712448 | bytes 40894464 | tf_op jit(solution)/shard_map/dot_general | solution.py:54
  74.7 0.2 convert.3
  75.1 0.7 collective-permute-start
  75.8 1.5 %collective-permute-done = bf16[16,8,2048]{2,1,0:T(8,128)(2,1)S(1)} collective-permute-done((bf16[16,8,2048]{2,1,0:T(8,128)(2,1)S(1)}, bf16[16,8,2048]{2,1,0:T(8,128)(2,1)S(1)}, u32[]{:S(2)}, u32[]{:S(2)}) %collective-permute-start) | collective-permute-done | bytes 524320 | tf_op jit(solution)/shard_map/ppermute | solution.py:18
  77.4 1.0 add_convert_fusion
  78.3 6.5 %all-to-all-start.2 = ((bf16[16,8,2048]{2,1,0:T(8,128)(2,1)}), bf16[16,8,2048]{2,1,0:T(8,128)(2,1)S(1)}, u32[]{:S(2)}, u32[]{:S(2)}) async-start(bf16[16,8,2048]{2,1,0:T(8,128)(2,1)} %add_convert_fusion), calls=%async_computation.2 | async-start | bytes 1048576 | tf_op jit(solution)/shard_map/all_to_all | solution.py:94
  85.2 13.9 %all-to-all-done.2 = bf16[16,8,2048]{2,1,0:T(8,128)(2,1)S(1)} async-done(((bf16[16,8,2048]{2,1,0:T(8,128)(2,1)}), bf16[16,8,2048]{2,1,0:T(8,128)(2,1)S(1)}, u32[]{:S(2)}, u32[]{:S(2)}) %all-to-all-start.2) | async-done | bytes 524320 | tf_op jit(solution)/shard_map/all_to_all | solution.py:94
  99.1 0.3 fusion.11
  99.4 0.4 fusion.2
  99.8 0.3 reshape.88
  100.1 1.3 %reduce_sum.32 = bf16[32,2048]{1,0:T(8,128)(2,1)} reduce(f32[32,2,2048]{2,1,0:T(2,128)S(1)} %reshape.88, f32[]{:T(128)} %constant.57.clone.1), dimensions={1}, to_apply=%region_3.4 | reduce | flops 65536 | bytes 655364 | tf_op jit(solution)/shard_map/reduce_sum | solution.py:161
  (30 shorter events, 1.5 us)
Async XLA Ops:
  0.0 22.5 %copy-start = (f32[8,8,4096]{2,1,0:T(8,128)S(1)}, f32[8,8,4096]{2,1,0:T(8,128)}, u32[]{:S(2)}) copy-start(f32[8,8,4096]{2,1,0:T(8,128)} %param.17) | copy-start | bytes 3145732
  0.0 22.4 %copy-start.3 = (f32[8,2,3584]{2,1,0:T(2,128)S(1)}, f32[8,2,3584]{2,1,0:T(2,128)}, u32[]{:S(2)}) copy-start(f32[8,2,3584]{2,1,0:T(2,128)} %param.18) | copy-start | bytes 688132
  3.8 13.8 %all-to-all-start.1 = ((bf16[16,16,1]{1,2,0:T(2,128)(2,1)}), bf16[16,16,1]{1,2,0:T(2,128)(2,1)S(1)}, u32[]{:S(2)}, u32[]{:S(2)}) async-start(bf16[16,16,1]{1,2,0:T(2,128)(2,1)} %copy.36), calls=%async_computation.1 | async-start | bytes 16384 | tf_op jit(solution)/shard_map/all_to_all | solution.py:138
  18.7 26.5 %all-to-all-start = ((bf16[16,16,2048]{2,1,0:T(8,128)(2,1)}), bf16[16,16,2048]{2,1,0:T(8,128)(2,1)S(1)}, u32[]{:S(2)}, u32[]{:S(2)}) async-start(bf16[16,16,2048]{2,1,0:T(8,128)(2,1)} %bitcast.1), calls=%async_computation | async-start | bytes 2097152 | tf_op jit(solution)/shard_map/all_to_all | solution.py:137
  75.0 9.9 %copy-start.5 = (f32[32,2]{0,1:T(2,128)S(1)}, f32[32,2]{0,1:T(2,128)}, u32[]{:S(2)}) copy-start(f32[32,2]{0,1:T(2,128)} %param.13) | copy-start | bytes 772
  75.0 10.1 %copy-start.4 = (s32[32]{0:T(128)S(1)}, s32[32]{0:T(128)}, u32[]{:S(2)}) copy-start(s32[32]{0:T(128)} %param.12) | copy-start | bytes 388
  75.0 24.4 %copy-start.2 = (f32[8,8,2048]{2,1,0:T(8,128)S(1)}, f32[8,8,2048]{2,1,0:T(8,128)}, u32[]{:S(2)}) copy-start(f32[8,8,2048]{2,1,0:T(8,128)} %param.19) | copy-start | bytes 1572868
  75.0 26.5 %copy-start.1 = (f32[8,8,4096]{2,1,0:T(8,128)S(1)}, f32[8,8,4096]{2,1,0:T(8,128)}, u32[]{:S(2)}) copy-start(f32[8,8,4096]{2,1,0:T(8,128)} %param.17) | copy-start | bytes 3145732
  75.1 2.3 %collective-permute-start = (bf16[16,8,2048]{2,1,0:T(8,128)(2,1)S(1)}, bf16[16,8,2048]{2,1,0:T(8,128)(2,1)S(1)}, u32[]{:S(2)}, u32[]{:S(2)}) collective-permute-start(bf16[16,8,2048]{2,1,0:T(8,128)(2,1)S(1)} %select_convert_fusion), channel_id=1, source_target_pairs={{0,1},{1,0},{2,3},{3,2},{4,5},{5,4},{6,7},{7,6},{8,9},{9,8},{10,11... | collective-permute-start | bytes 1572872 | tf_op jit(solution)/shard_map/ppermute | solution.py:18
  78.3 20.7 %all-to-all-start.2 = ((bf16[16,8,2048]{2,1,0:T(8,128)(2,1)}), bf16[16,8,2048]{2,1,0:T(8,128)(2,1)S(1)}, u32[]{:S(2)}, u32[]{:S(2)}) async-start(bf16[16,8,2048]{2,1,0:T(8,128)(2,1)} %add_convert_fusion), calls=%async_computation.2 | async-start | bytes 1048576 | tf_op jit(solution)/shard_map/all_to_all | solution.py:94
where the time goes:
time: 102 us; the launch traced here: 101 us
  matrix products  41.3 us (40%)
  waiting for transfers between devices  34.1 us (33%)
  starting transfers between devices  18.3 us (18%)
  other arithmetic  3.79 us (4%)
  local copies, waits for them, and re-layouts  3.78 us (4%)
    dot_general x1, matrix products, expert_rows(): jnp.dot(hidden, down_weight, preferred_element_type=jnp.float32)  16.9 us
    all_to_all x1, waiting for transfers between devices, send_back(): lax.all_to_all(held.astype(jnp.bfloat16), 'expert', split_axis=0, concat_...  13.9 us
    all_to_all x1, waiting for transfers between devices, per_device(): lax.all_to_all(rows_out, 'expert', split_axis=0, concat_axis=0, tiled=True)  13.6 us
    dot_general x1, matrix products, expert_rows(): gate = jnp.dot(gate_in, gate_weight, preferred_element_type=jnp.float32)  12.7 us
    dot_general x3, matrix products, lookup(): jnp.dot(select, table, precision=lax.Precision.HIGHEST, preferred_element...  9.45 us
    all_to_all x1, starting transfers between devices, per_device(): lax.all_to_all(member_out, 'expert', split_axis=0, concat_axis=0, tiled=T...  7.41 us
    all_to_all x1, starting transfers between devices, send_back(): lax.all_to_all(held.astype(jnp.bfloat16), 'expert', split_axis=0, concat_...  6.45 us
    all_to_all x1, waiting for transfers between devices, per_device(): lax.all_to_all(member_out, 'expert', split_axis=0, concat_axis=0, tiled=T...  5.13 us
  transfers between devices with their start and end apart: 4, of which 4 were waited for; matrix products, arithmetic and copies ran while one was open for 11% of the time, Pallas kernels for 0%

commit v1 on v0

v1 whole, which is shorter than its diff:
```python
import functools

import jax
import jax.numpy as jnp
from jax import lax
from jax.experimental import pallas as pl
from jax.experimental.pallas import tpu as pltpu
from jax.sharding import Mesh, PartitionSpec as P

EXPERTS = 8
MEMBERS = 8
CAP = 16
LANES = 128


def thirds(table):
    high = table.astype(jnp.bfloat16)
    rest = table - high.astype(jnp.float32)
    middle = rest.astype(jnp.bfloat16)
    low = (rest - middle.astype(jnp.float32)).astype(jnp.bfloat16)
    return jnp.concatenate([high, middle, low], axis=0)


def flag(condition):
    return jnp.where(condition, 1.0, 0.0)


def placing(ids):
    tok_count = ids.shape[1]
    slots = EXPERTS * CAP
    row = lax.broadcasted_iota(jnp.int32, (slots, tok_count), 0)
    expert = row // CAP
    first = ids[0:1, :] == expert
    second = ids[1:2, :] == expert
    named = flag(first) + flag(second)
    before = flag(
        lax.broadcasted_iota(jnp.int32, (tok_count, tok_count), 0)
        < lax.broadcasted_iota(jnp.int32, (tok_count, tok_count), 1)
    ).astype(jnp.bfloat16)
    rank = jnp.dot(named.astype(jnp.bfloat16), before, preferred_element_type=jnp.float32)
    here = rank == (row % CAP).astype(jnp.float32)
    return flag(first & here), flag(second & here)


def pack_kernel(tokens, ids, member_ids, rows):
    width = tokens.shape[1]
    first, second = placing(ids[...])
    chosen = first + second
    rows[:, :width] = jnp.dot(
        chosen.astype(jnp.bfloat16), tokens[...], preferred_element_type=jnp.float32
    ).astype(jnp.bfloat16)
    plus = (member_ids[...] + 1).astype(jnp.float32)
    member = jnp.sum(chosen * plus, axis=1, keepdims=True)
    rows[:, width:] = jnp.broadcast_to(member, (rows.shape[0], LANES)).astype(jnp.bfloat16)


def ffn_kernel(
    own_expert, rows, in_factors, hid_factors, gate_weight, up_weight, down_weight, partial_out,
    gate_in, up_in, select, total,
):
    step = pl.program_id(0)
    members = in_factors.shape[1]
    width = gate_in.shape[1]
    count = rows.shape[0]

    @pl.when(step == 0)
    def _():
        member = rows[:, width:width + 1].astype(jnp.float32) - 1.0
        column = lax.broadcasted_iota(jnp.int32, (count, 3 * members), 1) % members
        chosen = flag(member == column.astype(jnp.float32)).astype(jnp.bfloat16)
        select[...] = chosen
        scale = jnp.dot(chosen, thirds(in_factors[0]), preferred_element_type=jnp.float32)
        data = rows[:, :width].astype(jnp.float32)
        gate_in[...] = (data * scale[:, :width]).astype(jnp.bfloat16)
        up_in[...] = (data * scale[:, width:]).astype(jnp.bfloat16)

    chosen = select[...]
    gate_scale = jnp.dot(chosen, thirds(hid_factors[0]), preferred_element_type=jnp.float32)
    up_scale = jnp.dot(chosen, thirds(hid_factors[1]), preferred_element_type=jnp.float32)
    gate = jnp.dot(gate_in[...], gate_weight[...], preferred_element_type=jnp.float32) * gate_scale
    up = jnp.dot(up_in[...], up_weight[...], preferred_element_type=jnp.float32) * up_scale
    hidden = (gate / (1.0 + jnp.exp(-gate)) * up).astype(jnp.bfloat16)
    part = jnp.dot(hidden, down_weight[...], preferred_element_type=jnp.float32)

    @pl.when(step == 0)
    def _():
        total[...] = part

    @pl.when(step > 0)
    def _():
        total[...] = total[...] + part

    @pl.when(step == pl.num_programs(0) - 1)
    def _():
        partial_out[...] = total[...].astype(jnp.bfloat16)


def combine_kernel(summed, ids, member_ids, weights, out_factors, mixed):
    tok_count = ids.shape[1]
    table = thirds(out_factors[...])
    entries = out_factors.shape[0]
    spot = lax.broadcasted_iota(jnp.int32, (3 * entries, tok_count), 0) % entries
    diagonal = lax.broadcasted_iota(jnp.int32, (tok_count, tok_count), 0) == (
        lax.broadcasted_iota(jnp.int32, (tok_count, tok_count), 1)
    )
    over_rows = (((0,), (0,)), ((), ()))
    result = None
    for route, place in enumerate(placing(ids[...])):
        picked = lax.dot_general(
            place.astype(jnp.bfloat16), summed[...], over_rows, preferred_element_type=jnp.float32
        )
        entry = ids[route:route + 1, :] * MEMBERS + member_ids[...]
        chosen = flag(spot == entry).astype(jnp.bfloat16)
        scale = lax.dot_general(chosen, table, over_rows, preferred_element_type=jnp.float32)
        weight = jnp.sum(
            jnp.where(diagonal, weights[route:route + 1, :], 0.0), axis=1, keepdims=True
        )
        term = picked * scale * weight
        result = term if result is None else result + term
    mixed[...] = result.astype(jnp.bfloat16)


def block_of(units):
    best = LANES
    for block in range(LANES, 513, LANES):
        if units % block == 0:
            best = block
    return best


def run_rows(
    rows, own_expert, gate_weight, up_weight, down_weight, input_factors, hidden_factors
):
    count = rows.shape[0]
    width, units = gate_weight.shape
    members = input_factors.shape[1]
    block = block_of(units)
    spec = pltpu.PrefetchScalarGridSpec(
        num_scalar_prefetch=1,
        grid=(units // block,),
        in_specs=[
            pl.BlockSpec((count, rows.shape[1]), lambda i, own: (0, 0)),
            pl.BlockSpec((1, members, 2 * width), lambda i, own: (own[0], 0, 0)),
            pl.BlockSpec((2, members, block), lambda i, own: (0, 0, i)),
            pl.BlockSpec((width, block), lambda i, own: (0, i)),
            pl.BlockSpec((width, block), lambda i, own: (0, i)),
            pl.BlockSpec((block, width), lambda i, own: (i, 0)),
        ],
        out_specs=pl.BlockSpec((count, width), lambda i, own: (0, 0)),
        scratch_shapes=[
            pltpu.VMEM((count, width), jnp.bfloat16),
            pltpu.VMEM((count, width), jnp.bfloat16),
            pltpu.VMEM((count, 3 * members), jnp.bfloat16),
            pltpu.VMEM((count, width), jnp.float32),
        ],
    )
    return pl.pallas_call(
        ffn_kernel,
        grid_spec=spec,
        out_shape=jax.ShapeDtypeStruct((count, width), jnp.bfloat16),
        compiler_params=pltpu.CompilerParams(dimension_semantics=("arbitrary",)),
        name="ffn",
    )(
        own_expert, rows, input_factors, hidden_factors.transpose(1, 0, 2),
        gate_weight, up_weight, down_weight,
    )


def swapped(block, apart):
    count = lax.axis_size("share")
    route = [(place, place ^ apart) for place in range(count)]
    return lax.ppermute(block, "share", route)


def per_device(
    tokens,
    expert_ids,
    member_ids,
    combine_weights,
    gate_weight,
    up_weight,
    down_weight,
    input_factors,
    hidden_factors,
    output_factors,
):
    split = lax.axis_size("share")
    own_expert = lax.axis_index("owner").astype(jnp.int32).reshape(1)
    tok_count, width = tokens.shape
    slots = EXPERTS * CAP
    ids = expert_ids.T
    members = member_ids.reshape(1, tok_count)
    rows = pl.pallas_call(
        pack_kernel,
        out_shape=jax.ShapeDtypeStruct((slots, width + LANES), jnp.bfloat16),
        name="pack",
    )(tokens, ids, members)
    held = lax.all_to_all(
        rows.reshape(EXPERTS, CAP, width + LANES), "owner", split_axis=0, concat_axis=0, tiled=True
    ).reshape(slots, width + LANES)
    levels = split.bit_length() - 1
    for level in range(levels):
        held = jnp.concatenate([held, swapped(held, 1 << level)], axis=0)
    held = run_rows(
        held, own_expert, gate_weight, up_weight, down_weight, input_factors, hidden_factors
    )
    for level in reversed(range(levels)):
        half = held.shape[0] // 2
        other = swapped(held[half:], 1 << level)
        held = (held[:half].astype(jnp.float32) + other.astype(jnp.float32)).astype(jnp.bfloat16)
    summed = lax.all_to_all(
        held.reshape(EXPERTS, CAP, width), "owner", split_axis=0, concat_axis=0, tiled=True
    ).reshape(slots, width)
    return pl.pallas_call(
        combine_kernel,
        out_shape=jax.ShapeDtypeStruct((tok_count, width), jnp.bfloat16),
        name="combine",
    )(summed, ids, members, combine_weights.T, output_factors.reshape(EXPERTS * MEMBERS, width))


def solution(mesh):
    groups = mesh.shape["groups"]
    fine = Mesh(mesh.devices.reshape(groups, EXPERTS, -1), ("groups", "owner", "share"))
    expert = ("owner", "share")
    everyone = ("groups", "owner", "share")
    in_specs = (
        P(everyone, None),
        P(everyone, None),
        P(everyone),
        P(everyone, None),
        P(None, expert),
        P(None, expert),
        P(expert, None),
        P(),
        P(None, None, expert),
        P(),
    )
    return jax.shard_map(
        per_device, mesh=fine, in_specs=in_specs, out_specs=P(everyone, None), check_vma=False
    )
```

time: 102 us -> 77.1 us (0.76)
  blocking collectives: 0 us -> 41.5 us
  matrix products: 41.3 us -> 0 us
  waiting for transfers between devices: 34.1 us -> 1.91 us
  Pallas kernels: 0 us -> 27.9 us
  starting transfers between devices: 18.3 us -> 0.33 us
  other arithmetic: 3.79 us -> 2.24 us
    all_to_all x0 -> x2, blocking collectives: none -> 41.5 us  [the longest x1 23.3 us: per_device(): lax.all_to_all(rows.reshape(EXPERTS, CAP, width + LANES), 'owner', split_...]
    dot_general x8 -> x0, matrix products: 41.3 us -> none  [the longest x1 16.9 us: expert_rows(): jnp.dot(hidden, down_weight, preferred_element_type=jnp.float32)]
    all_to_all x3 -> x0, waiting for transfers between devices: 32.6 us -> none  [the longest x1 13.9 us: send_back(): lax.all_to_all(held.astype(jnp.bfloat16), 'expert', split_axis=0, concat_...]
    pallas_call x0 -> x3, Pallas kernels: none -> 27.9 us  [the longest x1 23.2 us: run_rows(): pl.pallas_call(ffn_kernel, grid_spec=spec, out_shape=jax.ShapeDtypeStruct...]
    all_to_all x3 -> x0, starting transfers between devices: 17.5 us -> none  [the longest x1 7.41 us: per_device(): lax.all_to_all(member_out, 'expert', split_axis=0, concat_axis=0, tiled=T...]
    broadcast_in_dim x4 -> x0, local copies, waits for them, and re-layouts: 1.79 us -> none  [the longest x1 1.09 us: per_device(): rows_out = jnp.repeat(send_rows.reshape(EXPERTS, CAP, width), split, axis=0)]
    reduce_sum x3 -> x0, other arithmetic: 1.6 us -> none  [the longest x1 1.34 us: per_device(): return weighted.reshape(tok_count, 2, width).sum(1).astype(jnp.bfloat16)]
    slice x0 -> x1, local copies, waits for them, and re-layouts: none -> 1.08 us  [per_device(): other = swapped(held[half:], 1 << level)]
  transfers between devices with their start and end apart: 4 -> 2, of which waited for: 4 -> 2; matrix products, arithmetic and copies ran while one was open for 11% -> 2% of each run, Pallas kernels for 0% -> 0%
where the time goes in v1:
time: 77.1 us; the launch traced here: 76.7 us
  blocking collectives  41.5 us (54%)
  Pallas kernels  27.9 us (36%)
  local copies, waits for them, and re-layouts  2.77 us (4%)
  other arithmetic  2.24 us (3%)
  waiting for transfers between devices  1.91 us (2%)
    all_to_all x1, blocking collectives, per_device(): lax.all_to_all(rows.reshape(EXPERTS, CAP, width + LANES), 'owner', split_...  23.3 us
    pallas_call x1, Pallas kernels, run_rows(): pl.pallas_call(ffn_kernel, grid_spec=spec, out_shape=jax.ShapeDtypeStruct...  23.2 us
    all_to_all x1, blocking collectives, per_device(): lax.all_to_all(held.reshape(EXPERTS, CAP, width), 'owner', split_axis=0,...  18.3 us
    pallas_call x1, Pallas kernels, per_device(): pl.pallas_call(combine_kernel, out_shape=jax.ShapeDtypeStruct((tok_count,...  2.62 us
    pallas_call x1, Pallas kernels, per_device(): pl.pallas_call(pack_kernel, out_shape=jax.ShapeDtypeStruct((slots, width...  2.11 us
    ppermute x2, waiting for transfers between devices, swapped(): return lax.ppermute(block, 'share', route)  1.91 us
    unnamed x1, local copies, waits for them, and re-layouts  1.69 us
  transfers between devices with their start and end apart: 2, of which 2 were waited for; matrix products, arithmetic and copies ran while one was open for 2% of the time, Pallas kernels for 0%

profile of v1, /device:TPU:0, one launch (start us, length us, event | category | flops | bytes accessed | tf_op | source)
XLA Modules:
  0.0 76.7 jit_solution(10527824911054012059)
XLA Ops:
  0.0 2.1 %pack.1 = bf16[128,2176]{1,0:T(8,128)(2,1)} custom-call(bf16[32,2048]{1,0:T(8,128)(2,1)} %tokens.1, s32[2,32]{1,0:T(2,128)} %bitcast.19, s32[1,32]{1,0:T(1,128)} %bitcast.21), custom_call_target="tpu_custom_call" | custom-call | tf_op jit(solution)/shard_map/pack/pallas_call | solution.py:193
  2.1 23.3 %all_to_all.10 = bf16[8,16,2176]{2,1,0:T(8,128)(2,1)S(1)} all-to-all(bf16[8,16,2176]{2,1,0:T(8,128)(2,1)} %bitcast.14), channel_id=1, replica_groups=mesh['groups'=2,'owner'=8,'share'=2] {'owner'}, dimensions={0} | all-to-all | bytes 1114112 | tf_op jit(solution)/shard_map/all_to_all | solution.py:198
  25.4 0.0 collective-permute-start
  25.4 1.7 %copy.13 = f32[8,2,3584]{2,0,1:T(8,128)} copy(f32[8,2,3584]{2,1,0:T(2,128)} %param.18) | data formatting | bytes 458752 | tf_op args[8]
  27.1 0.3 collective-permute-done
  27.3 1.1 %pad_maximum_fusion.rows = bf16[256,2176]{1,0:T(8,128)(2,1)} fusion(bf16[128,2176]{1,0:T(8,128)(2,1)S(1)} %collective-permute-done, bf16[128,2176]{1,0:T(8,128)(2,1)S(1)} %bitcast.13), kind=kLoop, calls=%fused_computation | loop fusion | flops 2228224 | bytes 2228224 | tf_op jit(solution)/shard_map/concatenate | solution.py:203
  28.4 23.2 %ffn.1 = bf16[256,2048]{1,0:T(8,128)(2,1)} custom-call(s32[1]{0:T(128)} %bitcast.own_expert, bf16[256,2176]{1,0:T(8,128)(2,1)} %pad_maximum_fusion.rows, f32[8,8,4096]{2,1,0:T(8,128)} %in_factors.1, f32[2,8,3584]{2,1,0:T(8,128)} %bitcast.17, bf16[2048,3584]{1,0:T(8,128)(2,1)} %gate_weight.1, bf16[2048,3584]{1,0:T(8,128)(2,1)} %up_weight.1, ...), custom_call_target="tpu_custom_call" | custom-call | tf_op jit(solution)/shard_map/ffn/pallas_call | solution.py:157
  51.6 1.1 %slice.9 = bf16[128,2048]{1,0:T(8,128)(2,1)S(1)} slice(bf16[256,2048]{1,0:T(8,128)(2,1)} %ffn.1), slice={[128:256], [0:2048]} | slice | bytes 1048576 | tf_op jit(solution)/shard_map/slice | solution.py:209
  52.7 0.3 collective-permute-start.1
  53.0 1.7 %collective-permute-done.1 = bf16[128,2048]{1,0:T(8,128)(2,1)S(1)} collective-permute-done((bf16[128,2048]{1,0:T(8,128)(2,1)S(1)}, bf16[128,2048]{1,0:T(8,128)(2,1)S(1)}, u32[]{:S(2)}, u32[]{:S(2)}) %collective-permute-start.1) | collective-permute-done | bytes 524320 | tf_op jit(solution)/shard_map/ppermute | solution.py:172
  54.7 1.2 %add_convert_fusion = bf16[128,2048]{1,0:T(8,128)(2,1)S(1)} fusion(bf16[128,2048]{1,0:T(8,128)(2,1)S(1)} %collective-permute-done.1, bf16[256,2048]{1,0:T(8,128)(2,1)} %ffn.1), kind=kLoop, calls=%fused_computation.1 | loop fusion | flops 1048576 | bytes 1572864 | tf_op jit(solution)/shard_map/convert_element_type | solution.py:210
  55.8 18.3 %all_to_all.11 = bf16[8,16,2048]{2,1,0:T(8,128)(2,1)} all-to-all(bf16[8,16,2048]{2,1,0:T(8,128)(2,1)S(1)} %bitcast.15), channel_id=1, replica_groups=mesh['groups'=2,'owner'=8,'share'=2] {'owner'}, dimensions={0} | all-to-all | bytes 1048576 | tf_op jit(solution)/shard_map/all_to_all | solution.py:211
  74.1 2.6 %combine.1 = bf16[32,2048]{1,0:T(8,128)(2,1)} custom-call(bf16[128,2048]{1,0:T(8,128)(2,1)} %bitcast.16, s32[2,32]{1,0:T(2,128)} %bitcast.20, s32[1,32]{1,0:T(1,128)} %bitcast.22, f32[2,32]{1,0:T(2,128)} %bitcast.23, f32[64,2048]{1,0:T(8,128)} %bitcast.18), custom_call_target="tpu_custom_call" | custom-call | tf_op jit(solution)/shard_map/combine/pallas_call | solution.py:214
Async XLA Ops:
  25.4 2.0 %collective-permute-start = (bf16[128,2176]{1,0:T(8,128)(2,1)S(1)}, bf16[128,2176]{1,0:T(8,128)(2,1)S(1)}, u32[]{:S(2)}, u32[]{:S(2)}) collective-permute-start(bf16[128,2176]{1,0:T(8,128)(2,1)S(1)} %bitcast.12), channel_id=1, source_target_pairs={{0,1},{1,0},{2,3},{3,2},{4,5},{5,4},{6,7},{7,6},{8,9},{9,8},{10,11... | collective-permute-start | bytes 1671176 | tf_op jit(solution)/shard_map/ppermute | solution.py:172
  52.7 2.0 %collective-permute-start.1 = (bf16[128,2048]{1,0:T(8,128)(2,1)S(1)}, bf16[128,2048]{1,0:T(8,128)(2,1)S(1)}, u32[]{:S(2)}, u32[]{:S(2)}) collective-permute-start(bf16[128,2048]{1,0:T(8,128)(2,1)S(1)} %slice.9), channel_id=1, source_target_pairs={{0,1},{1,0},{2,3},{3,2},{4,5},{5,4},{6,7},{7,6},{8,9},{9,8},{10,11... | collective-permute-start | bytes 1572872 | tf_op jit(solution)/shard_map/ppermute | solution.py:172
